TPU v7x, 32 devices: a whole 2x2x4 slice. The times are simulated.
32 devices in a mesh: band: 8 (over z, y), grid: 4 (over x, core).
Axes of the slice: x: 2, y: 2, z: 4, core: 2. Of those that a mesh axis runs over, the one named last changes fastest.
Arguments:
- orbitals: float32 [32, 110592], P('band', 'grid'), may hold values from -6 to 6
Outputs:
- exchange_vectors: float32 [32, 110592], P('band', 'grid')
- margin: float32 [32, 32], P('grid', 'band')
All inputs are finite; a program needn't handle non-finite values.
Results may differ from a plain program's by a relative error of at most 0.00012.
Values sent between devices are 32-bit elements; how exact they have to be, the bound alone decides.
A program may use at most 128 MiB of HBM per device.

v0:
```python
import functools

import jax
import jax.numpy as jnp
import numpy as np
from jax import lax
from jax.experimental import pallas as pl
from jax.experimental.pallas import tpu as pltpu
from jax.sharding import PartitionSpec as P


def kernel_values(ng):
    freqs = ((np.arange(ng) + ng // 2) % ng - ng // 2).astype(np.float32)
    sq = freqs[: ng // 2 + 1, None, None] ** 2 + freqs[None, :, None] ** 2 + freqs[None, None, :] ** 2
    safe = np.where(sq > 0, sq, np.float32(1.0))
    return np.where(sq > 0, 40.0 * (1.0 - np.exp(-sq / 16.0)) / safe, 0.0)


def hartley(ng):
    k = np.arange(ng)
    ang = (k[:, None] * k[None, :] % ng) * (2.0 * np.pi / ng)
    return np.cos(ang) + np.sin(ang)


def split_const(table):
    table = np.asarray(table, np.float32)
    hi = table.astype(jnp.bfloat16)
    lo = (table - hi.astype(np.float32)).astype(jnp.bfloat16)
    return hi, lo


def rfft(xs):
    n = len(xs)
    if n == 3:
        s = xs[1] + xs[2]
        d = xs[1] - xs[2]
        return [(xs[0] + s, None), (xs[0] - 0.5 * s, d * (-np.sqrt(3.0) / 2))]
    even, odd = rfft(xs[0::2]), rfft(xs[1::2])
    half = n // 2
    out = [None] * (half + 1)
    for k in range(half // 2 + 1):
        er, ei = even[k]
        orr, oi = odd[k]
        if k == 0:
            out[0] = (er + orr, None)
            out[half] = (er - orr, None)
            continue
        c, s = np.cos(2 * np.pi * k / n), -np.sin(2 * np.pi * k / n)
        if 2 * k == half:
            out[k] = (er, -orr)
            continue
        tr, ti = cmul(orr, oi, c, s)
        out[k] = (er + tr, addo(ei, ti))
        out[half - k] = (er - tr, subo(ti, ei))
    return out


def addo(a, b):
    return b if a is None else a + b


def subo(a, b):
    return a if b is None else a - b


def cmul(r, i, c, s):
    if i is None:
        return r * c, r * s
    if abs(abs(c) - abs(s)) < 1e-9:
        if s < 0 < c:
            return (r + i) * c, (i - r) * c
        return (r - i) * c, (r + i) * c
    return r * c - i * s, r * s + i * c


def irfft(spec, n):
    if n == 3:
        dc, (r, i) = spec[0][0], spec[1]
        base = dc - r
        t = i * np.sqrt(3.0)
        return [dc + 2.0 * r, base - t, base + t]
    half = n // 2
    even, odd = [None] * (half // 2 + 1), [None] * (half // 2 + 1)
    for k in range(half // 2 + 1):
        yr, yi = spec[k]
        if k == 0:
            hr = spec[half][0]
            even[0] = (yr + hr, None)
            odd[0] = (yr - hr, None)
            continue
        if 2 * k == half:
            even[k] = (yr + yr, None)
            odd[k] = (-(yi + yi), None)
            continue
        zr, zi = spec[half - k]
        er, ei = yr + zr, yi - zi
        dr, di = yr - zr, yi + zi
        c, s = np.cos(2 * np.pi * k / n), np.sin(2 * np.pi * k / n)
        even[k] = (er, ei)
        odd[k] = cmul(dr, di, c, s)
    ev, od = irfft(even, half), irfft(odd, half)
    out = [None] * n
    out[0::2], out[1::2] = ev, od
    return out


def split(v):
    hi = v.astype(jnp.bfloat16)
    lo = (v - hi.astype(jnp.float32)).astype(jnp.bfloat16)
    return hi, lo


def mm(a, b):
    return jnp.dot(a, b, preferred_element_type=jnp.float32)


def solve_kernel(ng, rows, a_ref, b_ref, k_ref, zh_ref, zl_ref, ty_ref, s_ref, o_ref, work):
    width = b_ref.shape[-1]
    owed_w = (o_ref.shape[-1] // (ng * 5)) * ng * 4
    out_w = o_ref.shape[-1]

    def ztrans(v):
        hi, lo = split(v)
        return mm(hi, zh_ref[...]) + mm(lo, zh_ref[...]) + mm(hi, zl_ref[...])

    def ytrans(v):
        hi, lo = split(v)
        return mm(ty_ref[...], jnp.concatenate([hi, lo, hi], axis=0))

    def forward(c, _):
        base = c * rows
        p = (a_ref[pl.ds(base, rows)] * b_ref[pl.ds(base, rows)]).reshape(rows * ng, width)
        q = ztrans(p).reshape(rows, ng, width)
        for r in range(rows):
            work[base + r] = ytrans(q[r])
        return 0

    lax.fori_loop(0, ng // rows, forward, 0)

    def xconv(t, _):
        y0 = pl.multiple_of(t * 8, 8)
        for l in range(width // 128):
            sl = (pl.ds(y0, 8), pl.ds(l * 128, 128))
            spec = rfft([work[x, sl[0], sl[1]] for x in range(ng)])
            out = []
            for k, (re, im) in enumerate(spec):
                kv = k_ref[k, sl[0], sl[1]]
                out.append((re * kv, None if im is None else im * kv))
            res = irfft(out, ng)
            for x in range(ng):
                work[x, sl[0], sl[1]] = res[x]
        return 0

    lax.fori_loop(0, ng // 8, xconv, 0)

    def inverse(c, _):
        base = c * rows
        q = jnp.concatenate([ytrans(work[base + r]) for r in range(rows)], axis=0)
        pot = ztrans(q)
        b = b_ref[pl.ds(base, rows)].reshape(rows * ng, width)
        a = a_ref[pl.ds(base, rows)].reshape(rows * ng, width)
        hi, lo = split(b * pot)
        vec = mm(hi, s_ref[...]) + mm(lo, s_ref[...])
        owed = a[:, :out_w] * pot[:, :out_w]
        lane = lax.broadcasted_iota(jnp.int32, owed.shape, 1)
        res = jnp.where(lane < owed_w, owed, vec)
        o_ref[pl.ds(base, rows)] = (-res).reshape(rows, ng, out_w)
        return 0

    lax.fori_loop(0, ng // rows, inverse, 0)


def solve(a, b, bands):
    ng, width = a.shape[0], a.shape[-1]
    count = width // ng
    ht = hartley(ng)
    th, tl = split_const(ht)
    zh, zl = split_const(np.kron(np.eye(count), ht))
    ty = np.concatenate([th, th, tl], axis=1)
    out_w = (bands + 1) * ng
    sel = np.zeros((width, out_w), np.float32)
    for p in range(count):
        sel[p * ng + np.arange(ng), bands * ng + np.arange(ng)] = 1.0
    kv = kernel_values(ng).astype(np.float32)
    kv = np.tile(kv / np.float32(ng**3), (1, 1, count))
    rows = 6
    return pl.pallas_call(
        functools.partial(solve_kernel, ng, rows),
        out_shape=jax.ShapeDtypeStruct((ng, ng, out_w), jnp.float32),
        in_specs=[pl.BlockSpec(memory_space=pltpu.VMEM)] * 7,
        out_specs=pl.BlockSpec(memory_space=pltpu.VMEM),
        scratch_shapes=[pltpu.VMEM((ng, ng, width), jnp.float32)],
        compiler_params=pltpu.CompilerParams(vmem_limit_bytes=56 * 1024 * 1024),
        cost_estimate=pl.CostEstimate(flops=10**10, bytes_accessed=10**7, transcendentals=0),
        name="solve",
    )(a, b, jnp.asarray(kv), jnp.asarray(zh), jnp.asarray(zl), jnp.asarray(ty), jnp.asarray(sel, jnp.bfloat16))


def from_behind(value, axis, steps):
    count = lax.axis_size(axis)
    return lax.ppermute(value, axis, [(s, (s + steps) % count) for s in range(count)])


def on_device(orbitals):
    groups = lax.axis_size("grid")
    bands, local = orbitals.shape
    ncell = local * groups
    ng = round(ncell ** (1 / 3))
    xs = local // (ng * ng)
    own = orbitals.reshape(bands, xs, ng, ng).transpose(1, 2, 0, 3).reshape(xs, ng, bands * ng)
    lower = from_behind(own, "band", 1)
    both = lax.all_gather(jnp.concatenate([lower, own], axis=2), "grid", axis=0, tiled=True)
    me = lax.axis_index("grid")
    mine = lax.dynamic_slice_in_dim(both, (bands + me) * ng, ng, axis=2)
    out = solve(jnp.tile(mine, (1, 1, 2 * bands)), both, bands)
    recv = lax.all_to_all(out.reshape(groups, xs, ng, -1), "grid", split_axis=0, concat_axis=0, tiled=True)
    owed = from_behind(recv[..., : bands * ng].sum(axis=0), "band", -1)
    vec = recv[..., bands * ng :] + owed.reshape(xs, ng, bands, ng).transpose(2, 0, 1, 3)
    vectors = vec.reshape(bands, local)
    terms = (
        lax.dot_general(
            lax.all_gather(orbitals, "band", axis=0, tiled=True),
            vectors,
            (((1,), (1,)), ((), ())),
            precision=lax.Precision.HIGHEST,
            preferred_element_type=jnp.float32,
        )
        / ncell
    )
    margin = lax.psum_scatter(terms, "grid", scatter_dimension=0, tiled=True)
    return (vectors, margin)


def solution(mesh):
    return jax.shard_map(
        on_device,
        mesh=mesh,
        in_specs=(P("band", "grid"),),
        out_specs=(P("band", "grid"), P("grid", "band")),
        check_vma=False,
    )
```

profile of v0, /device:TPU:0, one launch (start us, length us, event | category | flops | bytes accessed | tf_op | source)
XLA Modules:
  0.0 173.4 jit_solution(14870766596428895518)
XLA Ops:
  7.2 0.0 all-gather.4.cloned.1.call-start
  7.2 1.6 reshape.23
  8.8 0.8 copy.22
  9.5 0.5 reshape.24
  10.1 3.0 %collective-permute-start = (f32[12,48,192]{2,1,0:T(8,128)S(1)}, f32[12,48,192]{2,1,0:T(8,128)S(1)}, u32[]{:S(2)}, u32[]{:S(2)}) collective-permute-start(f32[12,48,192]{2,1,0:T(8,128)S(1)} %reshape.24), channel_id=1, source_target_pairs={{0,4},{4,8},{8,12},{12,16},{16,20},{20,24},{24,28},{28,0},{1,5},{5... | collective-permute-start | bytes 1327112 | tf_op jit(solution)/shard_map/ppermute | solution.py:201
  13.1 16.4 %collective-permute-done = f32[12,48,192]{2,1,0:T(8,128)S(1)} collective-permute-done((f32[12,48,192]{2,1,0:T(8,128)S(1)}, f32[12,48,192]{2,1,0:T(8,128)S(1)}, u32[]{:S(2)}, u32[]{:S(2)}) %collective-permute-start) | collective-permute-done | bytes 442400 | tf_op jit(solution)/shard_map/ppermute | solution.py:201
  29.5 1.1 pad_maximum_fusion
  30.6 0.0 all-gather.4.cloned.1.call-update
  30.6 0.0 all-gather.6.cloned.1.call-start
  30.7 0.7 all-gather.6.cloned.1.call-update
  31.4 28.6 %all-gather.4.cloned.1.call-done.b_ref = f32[48,48,384]{2,1,0:T(8,128)} async-done(((f32[12,48,384]{2,1,0:T(8,128)}), f32[48,48,384]{2,1,0:T(8,128)}) %all-gather.4.cloned.1.call-update) | async-done | bytes 3538960 | tf_op jit(solution)/shard_map/all_gather | solution.py:212
  60.0 2.0 %constant_dynamic-slice_fusion.1 = f32[48,48,48]{2,1,0:T(8,128)S(1)} fusion(f32[48,48,384]{2,1,0:T(8,128)} %all-gather.4.cloned.1.call-done.b_ref, s32[]{:T(128)S(6)} %select_n.3), kind=kLoop, calls=%fused_computation.7 | loop fusion | bytes 884740 | tf_op jit(solution)/shard_map/dynamic_slice | solution.py:214
  62.0 4.8 %tile.4 = f32[48,48,8,48]{3,2,1,0:T(8,128)} broadcast(f32[48,48,48]{2,1,0:T(8,128)S(1)} %constant_dynamic-slice_fusion.1), dimensions={0,1,3} | broadcast | bytes 3981312 | tf_op jit(solution)/shard_map/tile | solution.py:215
  66.8 8.4 %tile.10.a_ref = f32[48,48,384]{2,1,0:T(8,128)} reshape(f32[48,48,8,48]{3,2,1,0:T(8,128)} %tile.4) | data formatting | bytes 7077888 | tf_op jit(solution)/shard_map/tile | solution.py:215
  75.2 24.4 %solve.1 = f32[48,48,240]{2,1,0:T(8,128)} custom-call(f32[48,48,384]{2,1,0:T(8,128)} %tile.10.a_ref, f32[48,48,384]{2,1,0:T(8,128)} %all-gather.4.cloned.1.call-done.b_ref, f32[25,48,384]{2,1,0:T(8,128)} %constant.27.clone.k_ref, bf16[384,384]{1,0:T(8,128)(2,1)} %constant.28.clone.zh_ref, bf16[384,384]{1,0:T(8,128)(2,1)} %constant.29.clone.zl_ref, ...), custom_call_target="tpu_custom_call" | custom-call | flops 10000000000 | bytes 10000000 | tf_op jit(solution)/shard_map/solve/pallas_call | solution.py:187
  99.6 32.1 %all_to_all.5 = f32[4,12,48,240]{3,2,1,0:T(8,128)S(1)} all-to-all(f32[4,12,48,240]{3,2,1,0:T(8,128)} %bitcast.19), channel_id=1, replica_groups=mesh['band'=8,'grid'=4] {'grid'}, dimensions={0} | all-to-all | bytes 4423680 | tf_op jit(solution)/shard_map/all_to_all | solution.py:216
  131.7 1.1 slice_reduce_fusion
  132.8 4.2 %collective-permute-start.1 = (f32[12,48,192]{2,1,0:T(8,128)}, f32[12,48,192]{2,1,0:T(8,128)}, u32[]{:S(2)}, u32[]{:S(2)}) collective-permute-start(f32[12,48,192]{2,1,0:T(8,128)} %slice_reduce_fusion), channel_id=1, source_target_pairs={{0,28},{4,0},{8,4},{12,8},{16,12},{20,16},{24,20},{28,24},{1,29},{... | collective-permute-start | bytes 1327112 | tf_op jit(solution)/shard_map/ppermute | solution.py:201
  136.9 0.0 copy-done.1
  136.9 0.6 dynamic-slice
  138.2 0.0 all-gather.6.cloned.1.call-done
  138.2 3.9 %reshape.29 = f32[32,27648]{1,0:T(8,128)} reshape(f32[8,4,27648]{2,1,0:T(4,128)} %all-gather.6.cloned.1.call-done) | data formatting | bytes 7077888
  142.1 0.4 slice.8
  142.5 7.0 %collective-permute-done.1 = f32[12,48,192]{2,1,0:T(8,128)} collective-permute-done((f32[12,48,192]{2,1,0:T(8,128)}, f32[12,48,192]{2,1,0:T(8,128)}, u32[]{:S(2)}, u32[]{:S(2)}) %collective-permute-start.1) | collective-permute-done | bytes 442400 | tf_op jit(solution)/shard_map/ppermute | solution.py:201
  149.5 1.6 reshape.26
  151.1 0.9 copy_add_fusion
  152.0 1.1 copy.16
  153.2 3.2 %reshape.27 = f32[4,27648]{1,0:T(4,128)} reshape(f32[4,12,48,48]{3,2,1,0:T(8,128)} %copy.16) | data formatting | bytes 884736 | tf_op jit(solution)/shard_map/reshape | solution.py:219
  156.4 0.0 copy-done
  156.4 3.8 %fusion = f32[32,4]{0,1:T(4,128)S(1)} fusion(f32[4,27648]{1,0:T(4,128)} %reshape.27, f32[32,27648]{1,0:T(8,128)S(1)} %copy-done), kind=kOutput, calls=%fused_computation.4 | convolution fusion | flops 42467456 | bytes 3981824 | tf_op jit(solution)/shard_map/dot_general | solution.py:221
  160.2 5.7 %all-reduce = f32[32,4]{0,1:T(4,128)S(1)} all-reduce(f32[32,4]{0,1:T(4,128)S(1)} %fusion), channel_id=2, replica_groups=mesh['band'=8,'grid'=4] {'grid'}, use_global_device_ids=true, to_apply=%region_1.0.clone | all-reduce | flops 128 | bytes 1024
  165.9 0.7 constant_dynamic-slice_fusion
  (2 shorter events, 0.0 us)
Async XLA Ops:
  7.2 52.8 %all-gather.4.cloned.1.call-start = ((), (), s32[]{:S(2)}) async-start(), calls=%async_computation.1 | async-start | bytes 4423680 | tf_op jit(solution)/shard_map/all_gather | solution.py:212
  10.1 19.4 %collective-permute-start = (f32[12,48,192]{2,1,0:T(8,128)S(1)}, f32[12,48,192]{2,1,0:T(8,128)S(1)}, u32[]{:S(2)}, u32[]{:S(2)}) collective-permute-start(f32[12,48,192]{2,1,0:T(8,128)S(1)} %reshape.24), channel_id=1, source_target_pairs={{0,4},{4,8},{8,12},{12,16},{16,20},{20,24},{24,28},{28,0},{1,5},{5... | collective-permute-start | bytes 1327112 | tf_op jit(solution)/shard_map/ppermute | solution.py:201
  30.6 107.6 %all-gather.6.cloned.1.call-start = ((), (), s32[]{:S(2)}) async-start(), calls=%async_computation.2 | async-start | bytes 3981312 | tf_op jit(solution)/shard_map/all_gather | solution.py:222
  131.7 5.2 %copy-start.1 = (u32[32]{0:T(128)S(1)}, u32[32]{0:T(128)}, u32[]{:S(2)}) copy-start(u32[32]{0:T(128)} %constant.35) | copy-start | bytes 388
  132.8 16.7 %collective-permute-start.1 = (f32[12,48,192]{2,1,0:T(8,128)}, f32[12,48,192]{2,1,0:T(8,128)}, u32[]{:S(2)}, u32[]{:S(2)}) collective-permute-start(f32[12,48,192]{2,1,0:T(8,128)} %slice_reduce_fusion), channel_id=1, source_target_pairs={{0,28},{4,0},{8,4},{12,8},{16,12},{20,16},{24,20},{28,24},{1,29},{... | collective-permute-start | bytes 1327112 | tf_op jit(solution)/shard_map/ppermute | solution.py:201
  152.0 4.3 %copy-start = (f32[32,27648]{1,0:T(8,128)S(1)}, f32[32,27648]{1,0:T(8,128)}, u32[]{:S(2)}) copy-start(f32[32,27648]{1,0:T(8,128)} %reshape.29) | copy-start | bytes 10616836
Sparse Core Ops, SparseCore 0:
  30.8 29.1 all-gather.3
  62.1 64.6 all-gather.5
where the time goes:
time: 174 us; the launch traced here: 173 us
  waiting for transfers between devices  52.7 us (30%)
  blocking collectives  37.7 us (22%)
  local copies, waits for them, and re-layouts  29.6 us (17%)
  Pallas kernels  24.4 us (14%)
  between operations  14.8 us (9%)
  starting transfers between devices  7.31 us (4%)
  matrix products  3.85 us (2%)
  other arithmetic  3.1 us (2%)
    all_to_all x1, blocking collectives, on_device(): lax.all_to_all(out.reshape(groups, xs, ng, -1), 'grid', split_axis=0, con...  32.1 us
    all_gather x1, waiting for transfers between devices, on_device(): lax.all_gather(jnp.concatenate([lower, own], axis=2), 'grid', axis=0, til...  28.6 us
    pallas_call x1, Pallas kernels, solve(): pl.pallas_call(functools.partial(solve_kernel, ng, rows), out_shape=jax.S...  24.4 us
    ppermute x2, waiting for transfers between devices, from_behind(): lax.ppermute(value, axis, [(s, (s + steps) % count) for s in range(count)])  23.4 us
    another operation x2, local copies, waits for them, and re-layouts, on_device(): out = solve(jnp.tile(mine, (1, 1, 2 * bands)), both, bands)  13.2 us
    ppermute x2, starting transfers between devices, from_behind(): lax.ppermute(value, axis, [(s, (s + steps) % count) for s in range(count)])  7.24 us
    unnamed x1, blocking collectives  5.65 us
    unnamed x7, local copies, waits for them, and re-layouts  5.15 us
  transfers between devices with their start and end apart: 4, of which 3 were waited for; matrix products, arithmetic and copies ran while one was open for 12% of the time, Pallas kernels for 14%

commit v1 on v0

v1 whole, which is shorter than its diff:
```python
import functools

import jax
import jax.numpy as jnp
import numpy as np
from jax import lax
from jax.experimental import pallas as pl
from jax.experimental.pallas import tpu as pltpu
from jax.sharding import PartitionSpec as P


def kernel_values(ng):
    freqs = ((np.arange(ng) + ng // 2) % ng - ng // 2).astype(np.float32)
    sq = freqs[: ng // 2 + 1, None, None] ** 2 + freqs[None, :, None] ** 2 + freqs[None, None, :] ** 2
    safe = np.where(sq > 0, sq, np.float32(1.0))
    return np.where(sq > 0, 40.0 * (1.0 - np.exp(-sq / 16.0)) / safe, 0.0)


def hartley(ng):
    k = np.arange(ng)
    ang = (k[:, None] * k[None, :] % ng) * (2.0 * np.pi / ng)
    return np.cos(ang) + np.sin(ang)


def split_const(table):
    table = np.asarray(table, np.float32)
    hi = table.astype(jnp.bfloat16)
    lo = (table - hi.astype(np.float32)).astype(jnp.bfloat16)
    return hi, lo


def rfft(xs):
    n = len(xs)
    if n == 3:
        s = xs[1] + xs[2]
        d = xs[1] - xs[2]
        return [(xs[0] + s, None), (xs[0] - 0.5 * s, d * (-np.sqrt(3.0) / 2))]
    even, odd = rfft(xs[0::2]), rfft(xs[1::2])
    half = n // 2
    out = [None] * (half + 1)
    for k in range(half // 2 + 1):
        er, ei = even[k]
        orr, oi = odd[k]
        if k == 0:
            out[0] = (er + orr, None)
            out[half] = (er - orr, None)
            continue
        c, s = np.cos(2 * np.pi * k / n), -np.sin(2 * np.pi * k / n)
        if 2 * k == half:
            out[k] = (er, -orr)
            continue
        tr, ti = cmul(orr, oi, c, s)
        out[k] = (er + tr, addo(ei, ti))
        out[half - k] = (er - tr, subo(ti, ei))
    return out


def addo(a, b):
    return b if a is None else a + b


def subo(a, b):
    return a if b is None else a - b


def cmul(r, i, c, s):
    if i is None:
        return r * c, r * s
    if abs(abs(c) - abs(s)) < 1e-9:
        if s < 0 < c:
            return (r + i) * c, (i - r) * c
        return (r - i) * c, (r + i) * c
    return r * c - i * s, r * s + i * c


def irfft(spec, n):
    if n == 3:
        dc, (r, i) = spec[0][0], spec[1]
        base = dc - r
        t = i * np.sqrt(3.0)
        return [dc + 2.0 * r, base - t, base + t]
    half = n // 2
    even, odd = [None] * (half // 2 + 1), [None] * (half // 2 + 1)
    for k in range(half // 2 + 1):
        yr, yi = spec[k]
        if k == 0:
            hr = spec[half][0]
            even[0] = (yr + hr, None)
            odd[0] = (yr - hr, None)
            continue
        if 2 * k == half:
            even[k] = (yr + yr, None)
            odd[k] = (-(yi + yi), None)
            continue
        zr, zi = spec[half - k]
        er, ei = yr + zr, yi - zi
        dr, di = yr - zr, yi + zi
        c, s = np.cos(2 * np.pi * k / n), np.sin(2 * np.pi * k / n)
        even[k] = (er, ei)
        odd[k] = cmul(dr, di, c, s)
    ev, od = irfft(even, half), irfft(odd, half)
    out = [None] * n
    out[0::2], out[1::2] = ev, od
    return out


def split(v):
    hi = v.astype(jnp.bfloat16)
    lo = (v - hi.astype(jnp.float32)).astype(jnp.bfloat16)
    return hi, lo


def mm(a, b):
    return jnp.dot(a, b, preferred_element_type=jnp.float32)


def solve_kernel(ng, own_ref, k1_ref, k2_ref, zh_ref, zl_ref, ty_ref, sel_ref, s_ref, o_ref,
                 buf, amp, acc, work, vec, recv, rsem, ssem, nsem, osem, orsem, lsem):
    planes, _, width = own_ref.shape
    me = lax.axis_index("grid")
    band, nband = lax.axis_index("band"), lax.axis_size("band")
    chip, core = me // 2, me % 2
    sib = chip * 2 + (1 - core)
    cross = (1 - chip) * 2 + core
    far = (1 - chip) * 2 + (1 - core)
    above, below = (band + 1) % nband, (band + nband - 1) % nband
    mesh_id = pl.DeviceIdType.MESH

    def remote(src, dst, send, recv_sem, device):
        return pltpu.make_async_remote_copy(
            src_ref=src, dst_ref=dst, send_sem=send, recv_sem=recv_sem,
            device_id=device, device_id_type=mesh_id,
        )

    def share(blk, lane, slot, src, target):
        return remote(src, buf.at[blk, slot], ssem.at[blk, lane], rsem.at[blk, slot], (band, target))

    barrier = pltpu.get_barrier_semaphore()
    for device in ((band, sib), (band, cross), (band, far), (above, me), (below, me)):
        pl.semaphore_signal(barrier, inc=1, device_id=device, device_id_type=mesh_id)
    pl.semaphore_wait(barrier, 5)

    share(0, 1, me, own_ref, cross).start()
    share(0, 0, me, own_ref, sib).start()
    remote(own_ref, buf.at[1, me], nsem.at[0], rsem.at[1, me], (above, me)).start()
    remote(own_ref, buf.at[2, me], nsem.at[1], rsem.at[2, me], (below, me)).start()
    local = pltpu.make_async_copy(own_ref, buf.at[0, me], lsem)
    local.start()

    def arrived(blk, slot):
        share(blk, 0, slot, own_ref, sib).wait_recv()

    def relay(blk):
        arrived(blk, cross)
        share(blk, 2, cross, buf.at[blk, cross], sib).start()

    def spread(blk):
        arrived(blk, me)
        share(blk, 1, me, buf.at[blk, me], cross).start()
        share(blk, 0, me, buf.at[blk, me], sib).start()

    def ztrans(v):
        hi, lo = split(v)
        return mm(hi, zh_ref[...]) + mm(lo, zh_ref[...]) + mm(hi, zl_ref[...])

    def ytrans(v):
        hi, lo = split(v)
        return mm(ty_ref[...], jnp.concatenate([hi, lo, hi], axis=0))

    def slot_of(s):
        return ((chip + s // 2) % 2) * 2 + (core + s % 2) % 2

    def amplitude(slot):
        hi, lo = split(buf[0, slot].reshape(planes * ng, width))
        amp[slot] = (mm(hi, sel_ref[me]) + mm(lo, sel_ref[me])).reshape(planes, ng, width)

    def forward(blk, s):
        slot = slot_of(s)

        @pl.when(s == 1)
        def _():
            arrived(blk, sib)

        @pl.when(jnp.logical_and(blk == 0, s == 2))
        def _():
            relay(0)
            spread(1)

        @pl.when(s == 3)
        def _():
            arrived(blk, far)

        @pl.when(blk == 0)
        def _():
            amplitude(slot)

        p = (amp[slot] * buf[blk, slot]).reshape(planes * ng, width)
        q = ztrans(p).reshape(planes, ng, width)
        for r in range(planes):
            work[slot, r] = ytrans(q[r])

    def conv(vals, kern):
        spec = rfft(vals)
        out = []
        for k, (re, im) in enumerate(spec):
            kv = kern(k)
            out.append((re * kv, None if im is None else im * kv))
        return irfft(out, ng)

    def xconv(t):
        order = [(g, h, r) for g in range(4) for h in range(2) for r in range(planes)]
        for i in range(2):
            rows = pl.ds(pl.multiple_of(t * 16 + 8 * i, 8), 8)
            res = conv([work[g, r, rows, h * 128:h * 128 + 128] for g, h, r in order],
                       lambda k: k1_ref[k, rows, :])
            for (g, h, r), v in zip(order, res):
                work[g, r, rows, h * 128:h * 128 + 128] = v
        ra = pl.ds(pl.multiple_of(t * 16, 8), 8)
        rb = pl.ds(pl.multiple_of(t * 16 + 8, 8), 8)
        left = lax.broadcasted_iota(jnp.int32, (8, 128), 1) < 64

        def half(g, h, r):
            u, w = work[g, r, ra, 256:384], work[g, r, rb, 256:384]
            if h == 0:
                return jnp.where(left, u, pltpu.roll(w, 64, 1))
            return jnp.where(left, pltpu.roll(u, 64, 1), w)

        rk = pl.ds(pl.multiple_of(t * 8, 8), 8)
        res = dict(zip(order, conv([half(*o) for o in order], lambda k: k2_ref[k, rk, :])))
        for g in range(4):
            for r in range(planes):
                a, b = res[(g, 0, r)], res[(g, 1, r)]
                work[g, r, ra, 256:384] = jnp.where(left, a, pltpu.roll(b, 64, 1))
                work[g, r, rb, 256:384] = jnp.where(left, pltpu.roll(a, 64, 1), b)

    def push(slot):
        return remote(vec.at[slot], recv.at[me], osem.at[slot], orsem.at[me], (band, slot))

    def inverse(blk, s):
        slot = ((chip + 1 - s // 2) % 2) * 2 + (core + s % 2 + s // 2) % 2
        q = jnp.concatenate([ytrans(work[slot, r]) for r in range(planes)], axis=0)
        w = ztrans(q).reshape(planes, ng, width) * buf[blk, slot]

        @pl.when(blk == 0)
        def _():
            acc[slot] = w

        @pl.when(blk == 1)
        def _():
            acc[slot] += w

        @pl.when(blk == 2)
        def _():
            hi, lo = split((acc[slot] + w).reshape(planes * ng, width))
            out = -(mm(hi, s_ref[...]) + mm(lo, s_ref[...]))
            vec[slot] = out.reshape(planes, ng, s_ref.shape[-1])

            @pl.when(s < 3)
            def _():
                push(slot).start()

    def block(blk, _):
        @pl.when(blk == 0)
        def _():
            local.wait()

        @pl.when(blk > 0)
        def _():
            relay(blk)

        @pl.when(blk == 1)
        def _():
            spread(2)

        def fwd(s, _):
            forward(blk, s)
            return 0

        def mid(t, _):
            xconv(t)
            return 0

        def inv(s, _):
            inverse(blk, s)
            return 0

        lax.fori_loop(0, 4, fwd, 0)
        lax.fori_loop(0, ng // 16, mid, 0)
        lax.fori_loop(0, 4, inv, 0)
        return 0

    lax.fori_loop(0, 3, block, 0)

    o_ref[me] = vec[me]
    for slot in (sib, cross, far):
        remote(vec.at[slot], recv.at[slot], osem.at[slot], orsem.at[slot], (band, slot)).wait()
        o_ref[slot] = recv[slot]
    for blk in range(3):
        for lane, target in ((0, sib), (1, cross), (2, sib)):
            share(blk, lane, me, own_ref, target).wait_send()
    remote(own_ref, buf.at[1, me], nsem.at[0], rsem.at[1, me], (above, me)).wait_send()
    remote(own_ref, buf.at[2, me], nsem.at[1], rsem.at[2, me], (below, me)).wait_send()


def lane_tables(ng, bands):
    w = bands * ng
    half, bz = [], []
    for lo, hi in ((0, 128), (128, w)):
        for h in range(2):
            half.append(np.full(hi - lo, h))
            bz.append(np.arange(lo, hi))
    half, bz = np.concatenate(half), np.concatenate(bz)
    return half, bz // ng, bz % ng


def solve(own, bands, groups):
    planes, ng, width = own.shape
    half, bnd, zed = lane_tables(ng, bands)
    ht = hartley(ng)
    th, tl = split_const(ht)
    same = (half[:, None] == half[None, :])
    zh, zl = split_const(np.where(same & (bnd[:, None] == bnd[None, :]), ht[zed[:, None], zed[None, :]], 0.0))
    ty = np.concatenate([th, th, tl], axis=1)
    copyz = same & (zed[:, None] == zed[None, :])
    sel = np.stack([copyz & (bnd[:, None] == g) for g in range(groups)]).astype(np.float32)
    s = np.zeros((width, 128), np.float32)
    s[np.arange(width), half * ng + zed] = 1.0
    kv = kernel_values(ng).astype(np.float32) / np.float32(ng**3)
    kb = np.tile(kv, (1, 1, bands))
    k1 = kb[:, :, :128]
    rest = kb[:, :, 128:].reshape(kb.shape[0], ng // 16, 2, 8, 64)
    k2 = np.concatenate([rest[:, :, 0], rest[:, :, 1]], axis=-1).reshape(kb.shape[0], ng // 2, 128)
    consts = [k1, k2, zh, zl, ty, sel.astype(jnp.bfloat16), s.astype(jnp.bfloat16)]
    full = (groups, planes, ng, width)
    f32, dma = jnp.float32, pltpu.SemaphoreType.DMA
    return pl.pallas_call(
        functools.partial(solve_kernel, ng),
        out_shape=jax.ShapeDtypeStruct((groups, planes, ng, 128), f32),
        in_specs=[pl.BlockSpec(memory_space=pltpu.VMEM)] * 8,
        out_specs=pl.BlockSpec(memory_space=pltpu.VMEM),
        scratch_shapes=[
            pltpu.VMEM((3,) + full, f32), pltpu.VMEM(full, f32), pltpu.VMEM(full, f32), pltpu.VMEM(full, f32),
            pltpu.VMEM((groups, planes, ng, 128), f32), pltpu.VMEM((groups, planes, ng, 128), f32),
            dma((3, groups)), dma((3, 3)), dma((2,)), dma((groups,)), dma((groups,)), dma(()),
        ],
        compiler_params=pltpu.CompilerParams(
            vmem_limit_bytes=56 * 1024 * 1024, collective_id=0, has_side_effects=True
        ),
        cost_estimate=pl.CostEstimate(flops=10**11, bytes_accessed=10**7, transcendentals=0),
        name="solve",
    )(own, *[jnp.asarray(c) for c in consts])


def on_device(orbitals):
    groups = lax.axis_size("grid")
    bands, local = orbitals.shape
    ncell = local * groups
    ng = round(ncell ** (1 / 3))
    xs = local // (ng * ng)
    planes = xs // 2
    t = orbitals.reshape(bands, 2, planes, ng, ng).transpose(2, 3, 1, 0, 4).reshape(planes, ng, 2, bands * ng)
    own = jnp.concatenate([t[:, :, 0, :128], t[:, :, 1, :128], t[:, :, 0, 128:], t[:, :, 1, 128:]], axis=-1)
    out = solve(own, bands, groups)
    vec = out[..., : 2 * ng].reshape(groups, planes, ng, 2, ng).transpose(0, 3, 1, 2, 4)
    vectors = vec.reshape(bands, local)
    terms = (
        lax.dot_general(
            lax.all_gather(orbitals, "band", axis=0, tiled=True),
            vectors,
            (((1,), (1,)), ((), ())),
            precision=lax.Precision.HIGHEST,
            preferred_element_type=jnp.float32,
        )
        / ncell
    )
    margin = lax.psum_scatter(terms, "grid", scatter_dimension=0, tiled=True)
    return (vectors, margin)


def solution(mesh):
    return jax.shard_map(
        on_device,
        mesh=mesh,
        in_specs=(P("band", "grid"),),
        out_specs=(P("band", "grid"), P("grid", "band")),
        check_vma=False,
    )
```

time: 174 us -> 108 us (0.62)
  waiting for transfers between devices: 52.7 us -> 13.3 us
  Pallas kernels: 24.4 us -> 58.7 us
  blocking collectives: 37.7 us -> 5.65 us
  local copies, waits for them, and re-layouts: 29.6 us -> 10.3 us
  starting transfers between devices: 7.31 us -> 0.04 us
  other arithmetic: 3.1 us -> 0.87 us
    pallas_call x1, Pallas kernels: 24.4 us -> 58.7 us  [solve(): pl.pallas_call(functools.partial(solve_kernel, ng), out_shape=jax.ShapeDt...]
    all_to_all x1 -> x0, blocking collectives: 32.1 us -> none  [on_device(): lax.all_to_all(out.reshape(groups, xs, ng, -1), 'grid', split_axis=0, con...]
    all_gather x1 -> x0, waiting for transfers between devices: 28.6 us -> none  [on_device(): lax.all_gather(jnp.concatenate([lower, own], axis=2), 'grid', axis=0, til...]
    ppermute x2 -> x0, waiting for transfers between devices: 23.4 us -> none  [from_behind(): lax.ppermute(value, axis, [(s, (s + steps) % count) for s in range(count)])]
    another operation x2 -> x0, local copies, waits for them, and re-layouts: 13.2 us -> none  [on_device(): out = solve(jnp.tile(mine, (1, 1, 2 * bands)), both, bands)]
    all_gather x1, waiting for transfers between devices: 0.02 us -> 12.6 us  [on_device(): lax.all_gather(orbitals, 'band', axis=0, tiled=True)]
    ppermute x2 -> x0, starting transfers between devices: 7.24 us -> none  [from_behind(): lax.ppermute(value, axis, [(s, (s + steps) % count) for s in range(count)])]
    dynamic_slice x1 -> x0, local copies, waits for them, and re-layouts: 2.03 us -> none  [on_device(): mine = lax.dynamic_slice_in_dim(both, (bands + me) * ng, ng, axis=2)]
  transfers between devices with their start and end apart: 4 -> 1, of which waited for: 3 -> 1; matrix products, arithmetic and copies ran while one was open for 12% -> 7% of each run, Pallas kernels for 14% -> 55%
where the time goes in v1:
time: 108 us; the launch traced here: 107 us
  Pallas kernels  58.7 us (54%)
  between operations  14.8 us (14%)
  waiting for transfers between devices  13.3 us (12%)
  local copies, waits for them, and re-layouts  10.3 us (10%)
  blocking collectives  5.65 us (5%)
  matrix products  3.85 us (4%)
    pallas_call x1, Pallas kernels, solve(): pl.pallas_call(functools.partial(solve_kernel, ng), out_shape=jax.ShapeDt...  58.7 us
    all_gather x1, waiting for transfers between devices, on_device(): lax.all_gather(orbitals, 'band', axis=0, tiled=True)  12.6 us
    unnamed x1, blocking collectives  5.65 us
    unnamed x5, local copies, waits for them, and re-layouts  3.96 us
    dot_general x1, matrix products, on_device(): lax.dot_general(lax.all_gather(orbitals, 'band', axis=0, tiled=True), vec...  3.85 us
    reshape x3, local copies, waits for them, and re-layouts, on_device(): orbitals.reshape(bands, 2, planes, ng, ng).transpose(2, 3, 1, 0, 4)  2.84 us
  transfers between devices with their start and end apart: 1, of which 1 were waited for; matrix products, arithmetic and copies ran while one was open for 7% of the time, Pallas kernels for 55%

profile of v1, /device:TPU:0, one launch (start us, length us, event | category | flops | bytes accessed | tf_op | source)
XLA Modules:
  0.0 107.4 jit_solution(13691321328897510730)
XLA Ops:
  7.2 0.0 all-gather.3.cloned.1.call-start
  7.2 0.7 all-gather.3.cloned.1.call-update
  7.9 1.6 %reshape.16 = f32[4,2,6,48,48]{4,3,2,1,0:T(8,128)S(1)} reshape(f32[4,27648]{1,0:T(4,128)} %param.8) | data formatting | bytes 884736 | tf_op jit(solution)/shard_map/reshape | solution.py:361
  9.5 0.8 copy.17
  10.2 0.5 reshape.17
  10.8 0.9 pad_maximum_fusion.own_ref
  11.7 58.7 %solve.1 = f32[4,6,48,128]{3,2,1,0:T(8,128)} custom-call(f32[6,48,384]{2,1,0:T(8,128)} %pad_maximum_fusion.own_ref, f32[25,48,128]{2,1,0:T(8,128)} %constant.17.clone.k1_ref, f32[25,24,128]{2,1,0:T(8,128)} %constant.18.clone.k2_ref, bf16[384,384]{1,0:T(8,128)(2,1)} %constant.19.clone.zh_ref, bf16[384,384]{1,0:T(8,128)(2,1)} %constant.20.clone.zl_ref, ...), custom_call_target="tpu_custom_call" | custom-call | flops 99999997952 | bytes 10000000 | tf_op jit(solution)/shard_map/solve/pallas_call | solution.py:336
  70.4 0.0 copy-start
  70.4 1.7 %reshape.18 = f32[4,6,48,2,48]{4,3,2,1,0:T(2,128)S(1)} reshape(f32[4,6,48,96]{3,2,1,0:T(8,128)} %bitcast.30) | data formatting | bytes 884736 | tf_op jit(solution)/shard_map/reshape | solution.py:364
  72.1 0.1 copy.13
  72.2 1.6 %reshape.19 = f32[4,27648]{1,0:T(4,128)} reshape(f32[4,2,6,48,48]{4,3,2,1,0:T(8,128)S(1)} %copy.13) | data formatting | bytes 884736 | tf_op jit(solution)/shard_map/reshape | solution.py:365
  73.8 0.0 copy-done
  73.8 0.6 dynamic-slice
  75.0 12.6 %all-gather.3.cloned.1.call-done = f32[8,4,27648]{2,1,0:T(4,128)} async-done(((f32[1,4,27648]{2,1,0:T(4,128)}), f32[8,4,27648]{2,1,0:T(4,128)}) %all-gather.3.cloned.1.call-update) | async-done | bytes 3538960 | tf_op jit(solution)/shard_map/all_gather | solution.py:368
  87.7 2.7 %reshape.21 = f32[32,27648]{1,0:T(8,128)S(1)} reshape(f32[8,4,27648]{2,1,0:T(4,128)} %all-gather.3.cloned.1.call-done) | data formatting | bytes 7077888
  90.4 3.8 %fusion = f32[32,4]{0,1:T(4,128)S(1)} fusion(f32[4,27648]{1,0:T(4,128)} %reshape.19, f32[32,27648]{1,0:T(8,128)S(1)} %reshape.21), kind=kOutput, calls=%fused_computation.2 | convolution fusion | flops 42467456 | bytes 3981824 | tf_op jit(solution)/shard_map/dot_general | solution.py:367
  94.3 5.7 %all-reduce = f32[32,4]{0,1:T(4,128)S(1)} all-reduce(f32[32,4]{0,1:T(4,128)S(1)} %fusion), channel_id=2, replica_groups=mesh['band'=8,'grid'=4] {'grid'}, use_global_device_ids=true, to_apply=%region_0.0.clone | all-reduce | flops 128 | bytes 1024
  99.9 0.7 constant_dynamic-slice_fusion
  (2 shorter events, 0.0 us)
Async XLA Ops:
  7.2 80.5 %all-gather.3.cloned.1.call-start = ((), (), s32[]{:S(2)}) async-start(), calls=%async_computation | async-start | bytes 3981312 | tf_op jit(solution)/shard_map/all_gather | solution.py:368
  70.4 3.4 %copy-start = (u32[32]{0:T(128)S(1)}, u32[32]{0:T(128)}, u32[]{:S(2)}) copy-start(u32[32]{0:T(128)} %constant.27) | copy-start | bytes 388
Sparse Core Ops, SparseCore 0:
  10.2 77.4 all-gather.2
